TPU v7x, 256 devices: a whole 4x4x8 slice. The times are simulated.
256 devices in a mesh: dp: 128 (over z_hi, x, y, core), tensor: 2 (over z_lo).
Axes of the slice: x: 4, y: 4, z: 8 (z_hi: 4, z_lo: 2; z = z_hi * 2 + z_lo), core: 2. Of those that a mesh axis runs over, the one named last changes fastest.
Arguments:
- tokens: bfloat16 [16384, 1792], P('dp'), may hold values from -6 to 6
- targets: bfloat16 [16384, 1792], P('dp'), may hold values from -6 to 6
- live_mask: int32 [16384], P('dp'), may hold values from 0 to 1, as said below
- up_weight: bfloat16 [1792, 7168], P('dp', 'tensor'), may hold values from -0.125 to 0.125
- down_weight: bfloat16 [1792, 7168], P('dp', 'tensor'), may hold values from -0.0625 to 0.0625
- probe_rows: int32 [1792], replicated, may hold values from 0 to 16777215
- probe_cols: int32 [7168], P('tensor'), may hold values from 0 to 16777215
- moment: float32 [1792, 512], P('dp', 'tensor'), may hold values from 0.01 to 1
Outputs:
- hess_diag: float32 [1792, 512], P('dp', 'tensor')
- second_moment: float32 [1792, 512], P('dp', 'tensor')
- mean_loss: float32 [], replicated
Inputs may be any that keep to these rules, and one draw needn't show every extreme that they name: In every aligned block of 128 tokens the first token has live_mask 1.
All inputs are finite; a program needn't handle non-finite values.
Results may differ from a plain program's by a relative error of at most 0.0023.
Values may be sent and summed in bfloat16 or wider, within the bound.
No kernel may reach another device: no remote copies, remote signals or barrier semaphores. Data moves between devices by JAX's collectives and lax.ppermute only.
A program may use at most 128 MiB of HBM per device.

v0:
```python
import jax
import jax.numpy as jnp
from jax import lax
from jax.sharding import Mesh
from jax.sharding import PartitionSpec as P

BLOCK = 14
DP = ("dp_0", "dp_1", "dp_2", "dp_3")
DP_TENSOR = ("dp_0", "dp_1", "dp_2", "dp_3", "tensor")
gelu_coef = 0.7978845608028654
cubic_coef = 0.044715
beta_two = 0.999


def sent_to_all(shard, axis):
    copies = jnp.broadcast_to(shard, (lax.axis_size(axis), *shard.shape))
    return lax.all_to_all(copies, axis, split_axis=0, concat_axis=0, tiled=True)


def over_copies(shard, axis):
    everything = sent_to_all(shard, axis)
    return jnp.sum(everything, axis=0)


def together(arrays, axis):
    line, at, done = (jnp.concatenate([a.reshape(-1) for a in arrays]), 0, [])
    total = over_copies(line, axis)
    for a in arrays:
        done.append(total[at : at + a.size].reshape(a.shape))
        at += a.size
    return tuple(done)


def cut_along(shard, dim, count):
    before, after = (shard.shape[:dim], shard.shape[dim + 1 :])
    return jnp.moveaxis(shard.reshape(*before, count, -1, *after), dim, 0)


def sent_and_summed(shard, axis, dim):
    count = lax.axis_size(axis)
    tiles = lax.all_to_all(cut_along(shard, dim, count), axis, 0, 0, tiled=True)
    return jnp.sum(tiles, axis=0)


def sum_in_two_steps(shard, axes, dim):
    far, near = axes
    own = sent_and_summed(cut_along(shard, dim, lax.axis_size(far)), near, dim + 1)
    return jnp.sum(lax.all_to_all(own, far, 0, 0, tiled=True), axis=0)


def one_axis_at_a_time(shard, axes):
    for axis in axes:
        shard = lax.psum(shard, axis)
    return shard


def probe_signs(row_keys, col_keys):
    hashed = jnp.bitwise_xor(row_keys[:, None] * 747796405, col_keys[None, :])
    hashed = jnp.bitwise_xor(hashed, jnp.right_shift(hashed, 15) & 131071)
    hashed = hashed * 695872825
    hashed = jnp.bitwise_xor(hashed, jnp.right_shift(hashed, 13) & 524287)
    hashed = hashed * 739982445
    hashed = jnp.bitwise_xor(hashed, jnp.right_shift(hashed, 16) & 65535)
    parity = jnp.right_shift(hashed, 11) & 1
    return (2 * parity - 1).astype(jnp.bfloat16)


def gelu_parts(preact):
    tanh_arg = gelu_coef * (preact + cubic_coef * preact * preact * preact)
    tanh_val = jnp.tanh(tanh_arg)
    sech_sq = 1.0 - tanh_val * tanh_val
    arg_slope = gelu_coef * (1.0 + 3.0 * cubic_coef * preact * preact)
    arg_curve = gelu_coef * 6.0 * cubic_coef * preact
    gelu_value = 0.5 * preact * (1.0 + tanh_val)
    gelu_slope = 0.5 * (1.0 + tanh_val) + 0.5 * preact * sech_sq * arg_slope
    gelu_curve = sech_sq * (
        arg_slope - preact * tanh_val * arg_slope * arg_slope + 0.5 * preact * arg_curve
    )
    return (gelu_value, gelu_slope, gelu_curve)


def body(tokens, targets, live_mask, up_weight, down_weight, probe_rows, probe_cols, moment):
    tok_count = tokens.shape[0]
    ff_local = up_weight.shape[1]
    own_rows = up_weight.shape[0]
    tensor_count = lax.axis_size("tensor")
    live_rows = live_mask.astype(jnp.float32)
    local_count = jnp.sum(live_rows) * (1.0 / tensor_count)
    all_signs = probe_signs(probe_rows, probe_cols)
    columns = tokens
    sign_rows = all_signs
    joined = jnp.concatenate([lax.all_gather(up_weight, DP, axis=0, tiled=True), sign_rows], axis=1)
    both_pre = jnp.dot(columns, joined, preferred_element_type=jnp.float32)
    preact = both_pre[:, :ff_local]
    tangent = both_pre[:, ff_local:]
    full_down = lax.all_gather(down_weight, DP, axis=0, tiled=True)
    gelu_value, gelu_slope, gelu_curve = gelu_parts(preact)
    hidden = gelu_value.astype(jnp.bfloat16)
    hidden_dir = (gelu_slope * tangent).astype(jnp.bfloat16)
    stacked = jnp.concatenate([hidden, hidden_dir], axis=0)
    projected = jnp.einsum("tf,df->td", stacked, full_down, preferred_element_type=jnp.float32)
    outputs, out_dir = together((projected[:tok_count], projected[tok_count:]), "tensor")
    diff = outputs - targets.astype(jnp.float32)
    weighted = live_rows[:, None] * diff
    local_loss = jnp.sum(weighted * diff) * (1.0 / tensor_count)
    residual = weighted.astype(jnp.bfloat16)
    residual_dir = (live_rows[:, None] * out_dir).astype(jnp.bfloat16)
    back_prod = jnp.dot(
        jnp.concatenate([residual, residual_dir], axis=0),
        full_down,
        preferred_element_type=jnp.float32,
    )
    grad_h = back_prod[:tok_count]
    grad_dir = back_prod[tok_count:]
    chain_grad = (grad_dir * gelu_slope + grad_h * gelu_curve * tangent).astype(jnp.bfloat16)
    columns = tokens
    product = jnp.einsum("tr,tf->rf", columns, chain_grad, preferred_element_type=jnp.float32)
    sign_rows = all_signs
    hutch_terms = sign_rows.astype(jnp.float32) * product
    own_share = sum_in_two_steps(
        hutch_terms.reshape(own_rows * lax.axis_size(DP), ff_local // BLOCK, BLOCK).mean(axis=-1),
        (("dp_0", "dp_1", "dp_2"), "dp_3"),
        0,
    )
    loss_sum, total_count = (
        one_axis_at_a_time(local_loss, DP_TENSOR),
        one_axis_at_a_time(local_count, DP_TENSOR),
    )
    hess_diag = own_share / total_count
    second_moment = beta_two * moment + (1.0 - beta_two) * hess_diag * hess_diag
    mean_loss = loss_sum / (2.0 * total_count)
    return (hess_diag, second_moment, mean_loss)


def solution(mesh):
    torus = Mesh(
        mesh.devices.reshape(4, 4, 4, 2, mesh.shape["tensor"]),
        ("dp_0", "dp_1", "dp_2", "dp_3", "tensor"),
    )
    placed = (
        P(DP, None),
        P(DP, None),
        P(DP),
        P(DP, "tensor"),
        P(DP, "tensor"),
        P(),
        P("tensor"),
        P(DP, "tensor"),
    )
    return jax.shard_map(
        body,
        mesh=torus,
        in_specs=placed,
        out_specs=(P(DP, "tensor"), P(DP, "tensor"), P()),
        check_vma=False,
    )
```

profile of v0, /device:TPU:1, one launch (start us, length us, event | category | flops | bytes accessed | tf_op | source)
XLA Modules:
  0.0 491.9 jit_solution(3638978809061497128)
XLA Ops:
  7.2 0.0 copy-start
  7.2 0.0 all-gather.5.cloned.1.call-start
  7.2 0.7 all-gather.5.cloned.1.call-update
  7.9 0.0 all-gather.7.cloned.1.call-start
  8.0 0.7 all-gather.7.cloned.1.call-update
  8.7 0.7 broadcast_multiply_fusion.1
  9.4 15.8 %add_convert_fusion = bf16[1792,3584]{0,1:T(8,128)(2,1)} fusion(s32[3584]{0:T(1024)} %param.14, s32[1792]{0:T(1024)S(1)} %broadcast_multiply_fusion.1), kind=kLoop, calls=%fused_computation.13 | loop fusion | flops 109182976 | bytes 12866560 | tf_op jit(solution)/shard_map/convert_element_type | solution.py:65
  25.2 99.8 %all-gather.5.cloned.1.call-done = bf16[128,14,3584]{2,1,0:T(8,128)(2,1)} async-done(((bf16[1,14,3584]{2,1,0:T(8,128)(2,1)}), bf16[128,14,3584]{2,1,0:T(8,128)(2,1)}) %all-gather.5.cloned.1.call-update) | async-done | bytes 12845072 | tf_op jit(solution)/shard_map/all_gather | solution.py:92
  125.0 16.8 %reshape.48 = bf16[1792,3584]{1,0:T(8,128)(2,1)} reshape(bf16[128,14,3584]{2,1,0:T(8,128)(2,1)} %all-gather.5.cloned.1.call-done) | data formatting | bytes 25690112
  141.9 17.9 %copy.27 = bf16[1792,3584]{0,1:T(8,128)(2,1)} copy(bf16[1792,3584]{1,0:T(8,128)(2,1)} %reshape.48) | data formatting | bytes 25690112
  159.8 15.2 %fusion.10 = f32[128,7168]{1,0:T(8,128)} fusion(bf16[128,1792]{1,0:T(8,128)(2,1)S(1)} %copy-done, bf16[1792,3584]{0,1:T(8,128)(2,1)} %add_convert_fusion, bf16[1792,3584]{0,1:T(8,128)(2,1)} %copy.27), kind=kOutput, calls=%fused_computation.14 | convolution fusion | flops 3339714560 | bytes 29818880 | tf_op jit(solution)/shard_map/dot_general | solution.py:93
  175.0 3.3 multiply_convert_fusion.1
  178.3 57.5 %all-gather.7.cloned.1.call-done = bf16[128,14,3584]{2,1,0:T(8,128)(2,1)} async-done(((bf16[1,14,3584]{2,1,0:T(8,128)(2,1)}), bf16[128,14,3584]{2,1,0:T(8,128)(2,1)}) %all-gather.7.cloned.1.call-update) | async-done | bytes 12845072 | tf_op jit(solution)/shard_map/all_gather | solution.py:96
  235.8 16.8 %reshape.50 = bf16[1792,3584]{1,0:T(8,128)(2,1)} reshape(bf16[128,14,3584]{2,1,0:T(8,128)(2,1)} %all-gather.7.cloned.1.call-done) | data formatting | bytes 25690112
  252.6 7.0 %fusion.23 = f32[256,1792]{1,0:T(8,128)S(1)} fusion(bf16[1792,3584]{1,0:T(8,128)(2,1)} %reshape.50, bf16[128,3584]{1,0:T(8,128)(2,1)S(1)} %get-tuple-element.16, bf16[128,3584]{1,0:T(8,128)(2,1)S(1)} %get-tuple-element.15), kind=kOutput, calls=%fused_computation.29 | convolution fusion | flops 3292004352 | bytes 16515072 | tf_op jit(solution)/shard_map/tf,df->td/dot_general | solution.py:101
  259.7 0.1 fusion.50
  259.8 0.1 reshape.45
  259.9 0.1 reshape.44
  259.9 0.1 pad_maximum_fusion
  260.1 3.3 broadcast_in_dim.2
  263.3 5.7 %all-to-all-start = ((f32[2,1,458752]{2,1,0:T(1,128)}), f32[2,1,458752]{2,1,0:T(1,128)}, u32[]{:S(2)}, u32[]{:S(2)}) async-start(f32[2,1,458752]{2,1,0:T(1,128)} %broadcast_in_dim.2), calls=%async_computation | async-start | bytes 7340032 | tf_op jit(solution)/shard_map/all_to_all | solution.py:17
  269.1 41.4 %all-to-all-done = f32[2,1,458752]{2,1,0:T(1,128)} async-done(((f32[2,1,458752]{2,1,0:T(1,128)}), f32[2,1,458752]{2,1,0:T(1,128)}, u32[]{:S(2)}, u32[]{:S(2)}) %all-to-all-start) | async-done | bytes 3670048 | tf_op jit(solution)/shard_map/all_to_all | solution.py:17
  310.5 18.1 %reduce_sum.54 = f32[458752]{0:T(1024)S(1)} reduce(f32[2,1,458752]{2,1,0:T(1,128)} %all-to-all-done, f32[]{:T(128)} %constant.20.clone.1), dimensions={0,1}, to_apply=%region_0.0 | reduce | flops 458752 | bytes 5505028 | tf_op jit(solution)/shard_map/reduce_sum | solution.py:22
  328.6 1.0 fusion.49
  329.7 1.3 slice.49
  331.0 0.2 slice.51
  331.2 2.0 fusion.27
  333.1 6.7 %fusion.29 = f32[256,3584]{1,0:T(8,128)S(1)} fusion(bf16[1792,3584]{1,0:T(8,128)(2,1)} %reshape.50, bf16[128,1792]{1,0:T(8,128)(2,1)S(1)} %get-tuple-element.23, bf16[128,1792]{1,0:T(8,128)(2,1)S(1)} %get-tuple-element.22), kind=kOutput, calls=%fused_computation.41 | convolution fusion | flops 3290169344 | bytes 17432576 | tf_op jit(solution)/shard_map/dot_general | solution.py:108
  339.8 17.9 %bitcast_multiply_fusion = f32[1792,3584]{0,1:T(8,128)} fusion(bf16[128,1792]{1,0:T(8,128)(2,1)S(1)} %copy-done, s32[3584]{0:T(1024)S(1)} %copy-done.3, s32[1792]{0:T(1024)S(1)} %broadcast_multiply_fusion.1, f32[256,3584]{1,0:T(8,128)S(1)} %fusion.29, f32[128,7168]{1,0:T(8,128)S(1)} %copy-done.2), kind=kOutput, calls=%fused_computation.12 | convolution fusion | flops 1779957760 | bytes 33510400 | tf_op jit(solution)/shard_map/tr,tf->rf/dot_general | solution.py:117
  357.7 26.7 %reshape.46 = f32[1792,256,14]{0,2,1:T(8,128)} reshape(f32[1792,3584]{0,1:T(8,128)} %bitcast_multiply_fusion) | data formatting | bytes 51380224 | tf_op jit(solution)/shard_map/reshape | solution.py:121
  384.4 13.6 %reduce_sum.55 = f32[1792,256]{0,1:T(8,128)} reduce(f32[1792,256,14]{0,2,1:T(8,128)} %reshape.46, f32[]{:T(128)} %constant.20.clone.1), dimensions={2}, to_apply=%region_1.0 | reduce | flops 5963776 | bytes 27525124 | tf_op jit(solution)/shard_map/reduce_sum | solution.py:121
  398.0 1.7 broadcast_multiply_fusion
  399.7 1.7 copy.29
  401.4 1.6 div.19
  403.0 1.1 copy.30
  404.1 0.0 copy-start.1
  404.1 6.1 %all_to_all.16 = f32[2,64,14,256]{3,1,2,0:T(8,128)S(1)} all-to-all(f32[2,64,14,256]{3,1,2,0:T(8,128)S(1)} %copy.30), channel_id=1, replica_groups=mesh['dp_0'=4,'dp_1'=4,'dp_2'=4,'dp_3'=2,'tensor'=2] {'dp_3'}, dimensions={0} | all-to-all | bytes 3670016 | tf_op jit(solution)/shard_map/all_to_all | solution.py:41
  410.2 0.2 reduce_sum.56
  410.4 1.5 copy.31
  411.9 9.3 %all-to-all-start.2 = ((f32[64,14,256]{2,1,0:T(8,128)}), f32[64,14,256]{2,1,0:T(8,128)S(1)}, u32[]{:S(2)}, u32[]{:S(2)}) async-start(f32[64,14,256]{2,1,0:T(8,128)} %copy.31), calls=%async_computation.2 | async-start | bytes 2097152 | tf_op jit(solution)/shard_map/all_to_all | solution.py:48
  421.2 0.6 convert_reduce_fusion
  423.1 26.9 %all-reduce.2 = (f32[]{:T(128)}, f32[]{:T(128)}) all-reduce(f32[]{:T(128)S(6)} %mul.184, f32[]{:T(128)S(6)} %mul.191), channel_id=1, replica_groups=mesh['dp_0'=4,'dp_1'=4,'dp_2'=4,'dp_3'=2,'tensor'=2] {'dp_0'}, use_global_device_ids=true, to_apply=%region_5.0 | all-reduce | flops 2 | bytes 16 | tf_op jit(solution)/shard_map/psum | solution.py:53
  450.1 8.9 %all-reduce.1 = (f32[]{:T(128)}, f32[]{:T(128)}) all-reduce(f32[]{:T(128)} %get-tuple-element.7, f32[]{:T(128)} %get-tuple-element.8), channel_id=1, replica_groups=mesh['dp_0'=4,'dp_1'=4,'dp_2'=4,'dp_3'=2,'tensor'=2] {'dp_1'}, use_global_device_ids=true, to_apply=%region_6.0 | all-reduce | flops 2 | bytes 16 | tf_op jit(solution)/shard_map/psum | solution.py:53
  459.0 8.8 %all-reduce = (f32[]{:T(128)}, f32[]{:T(128)}) all-reduce(f32[]{:T(128)} %get-tuple-element.5, f32[]{:T(128)} %get-tuple-element.6), channel_id=1, replica_groups=mesh['dp_0'=4,'dp_1'=4,'dp_2'=4,'dp_3'=2,'tensor'=2] {'dp_2'}, use_global_device_ids=true, to_apply=%region_7.0 | all-reduce | flops 2 | bytes 16 | tf_op jit(solution)/shard_map/psum | solution.py:53
  467.8 8.8 %all-reduce.4 = (f32[]{:T(128)}, f32[]{:T(128)}) all-reduce(f32[]{:T(128)} %get-tuple-element.3, f32[]{:T(128)} %get-tuple-element.4), channel_id=1, replica_groups=mesh['dp_0'=4,'dp_1'=4,'dp_2'=4,'dp_3'=2,'tensor'=2] {'dp_3'}, use_global_device_ids=true, to_apply=%region_8.0 | all-reduce | flops 2 | bytes 16 | tf_op jit(solution)/shard_map/psum | solution.py:53
  476.5 4.6 all-reduce.3
  482.5 0.1 reduce_sum.57
  482.7 1.3 fusion.39
  (12 shorter events, 0.0 us)
Async XLA Ops:
  7.2 152.6 %copy-start = (bf16[128,1792]{1,0:T(8,128)(2,1)S(1)}, bf16[128,1792]{1,0:T(8,128)(2,1)}, u32[]{:S(2)}) copy-start(bf16[128,1792]{1,0:T(8,128)(2,1)} %param.8) | copy-start | bytes 1376260
  7.2 117.9 %all-gather.5.cloned.1.call-start = ((), (), s32[]{:S(2)}) async-start(), calls=%async_computation.3 | async-start | bytes 14794752 | tf_op jit(solution)/shard_map/all_gather | solution.py:92
  7.9 227.9 %all-gather.7.cloned.1.call-start = ((), (), s32[]{:S(2)}) async-start(), calls=%async_computation.4 | async-start | bytes 14794752 | tf_op jit(solution)/shard_map/all_gather | solution.py:96
  263.3 5.7 %copy-start.5 = (s32[128]{0:T(128)S(1)}, s32[128]{0:T(128)}, u32[]{:S(2)}) copy-start(s32[128]{0:T(128)} %param.10) | copy-start | bytes 1540
  263.3 47.2 %all-to-all-start = ((f32[2,1,458752]{2,1,0:T(1,128)}), f32[2,1,458752]{2,1,0:T(1,128)}, u32[]{:S(2)}, u32[]{:S(2)}) async-start(f32[2,1,458752]{2,1,0:T(1,128)} %broadcast_in_dim.2), calls=%async_computation | async-start | bytes 7340032 | tf_op jit(solution)/shard_map/all_to_all | solution.py:17
  333.1 6.7 %copy-start.2 = (f32[128,7168]{1,0:T(8,128)S(1)}, f32[128,7168]{1,0:T(8,128)}, u32[]{:S(2)}) copy-start(f32[128,7168]{1,0:T(8,128)} %fusion.10) | copy-start | bytes 11010052
  333.1 6.7 %copy-start.3 = (s32[3584]{0:T(1024)S(1)}, s32[3584]{0:T(1024)}, u32[]{:S(2)}) copy-start(s32[3584]{0:T(1024)} %param.14) | copy-start | bytes 43012
  404.1 79.9 %copy-start.1 = (bf16[128,1792]{1,0:T(8,128)(2,1)S(1)}, bf16[128,1792]{1,0:T(8,128)(2,1)}, u32[]{:S(2)}) copy-start(bf16[128,1792]{1,0:T(8,128)(2,1)} %param.8) | copy-start | bytes 1376260
  410.2 72.5 %copy-start.4 = (f32[14,256]{1,0:T(8,128)S(1)}, f32[14,256]{1,0:T(8,128)}, u32[]{:S(2)}) copy-start(f32[14,256]{1,0:T(8,128)} %param.15) | copy-start | bytes 43012
  411.9 70.6 %all-to-all-start.2 = ((f32[64,14,256]{2,1,0:T(8,128)}), f32[64,14,256]{2,1,0:T(8,128)S(1)}, u32[]{:S(2)}, u32[]{:S(2)}) async-start(f32[64,14,256]{2,1,0:T(8,128)} %copy.31), calls=%async_computation.2 | async-start | bytes 2097152 | tf_op jit(solution)/shard_map/all_to_all | solution.py:48
Sparse Core Ops, SparseCore 0:
  11.4 113.6 all-gather.4
  128.5 107.3 all-gather.6
where the time goes:
time: 495 us; the launch traced here: 492 us
  waiting for transfers between devices  200 us (40%)
  local copies, waits for them, and re-layouts  90.2 us (18%)
  blocking collectives  64.2 us (13%)
  other arithmetic  57.6 us (12%)
  matrix products  46.8 us (9%)
  between operations  18 us (4%)
  starting transfers between devices  15.1 us (3%)
    all_gather x1, waiting for transfers between devices, body(): lax.all_gather(up_weight, DP, axis=0, tiled=True)  99.8 us
    psum x5, blocking collectives, one_axis_at_a_time(): shard = lax.psum(shard, axis)  58.1 us
    all_gather x1, waiting for transfers between devices, body(): full_down = lax.all_gather(down_weight, DP, axis=0, tiled=True)  57.5 us
    unnamed x15, local copies, waits for them, and re-layouts  51.6 us
    all_to_all x1, waiting for transfers between devices, sent_to_all(): return lax.all_to_all(copies, axis, split_axis=0, concat_axis=0, tiled=True)  41.4 us
    reshape x1, local copies, waits for them, and re-layouts, body(): hutch_terms.reshape(own_rows * lax.axis_size(DP), ff_local // BLOCK, BLOCK)  26.7 us
    reduce_sum x1, other arithmetic, over_copies(): return jnp.sum(everything, axis=0)  18.1 us
    dot_general x1, matrix products, body(): jnp.einsum('tr,tf->rf', columns, chain_grad, preferred_element_type=jnp.f...  17.9 us
  transfers between devices with their start and end apart: 4, of which 3 were waited for; matrix products, arithmetic and copies ran while one was open for 14% of the time, Pallas kernels for 0%

commit v1 on v0

--- a/solution.py
+++ b/solution.py
@@ -93,7 +93,8 @@
     both_pre = jnp.dot(columns, joined, preferred_element_type=jnp.float32)
     preact = both_pre[:, :ff_local]
     tangent = both_pre[:, ff_local:]
-    full_down = lax.all_gather(down_weight, DP, axis=0, tiled=True)
+    repeated = jnp.stack([down_weight] * lax.axis_size(DP))
+    full_down = jnp.concatenate(lax.all_to_all(repeated, DP, 0, 0), axis=0)
     gelu_value, gelu_slope, gelu_curve = gelu_parts(preact)
     hidden = gelu_value.astype(jnp.bfloat16)
     hidden_dir = (gelu_slope * tangent).astype(jnp.bfloat16)

time: 495 us -> 714 us (1.44)
  waiting for transfers between devices: 200 us -> 351 us
  starting transfers between devices: 15.1 us -> 76.5 us
  local copies, waits for them, and re-layouts: 90.2 us -> 98.1 us
    all_gather x1, waiting for transfers between devices: 99.8 us -> 251 us  [body(): lax.all_gather(up_weight, DP, axis=0, tiled=True)]
    all_to_all x0 -> x1, waiting for transfers between devices: none -> 58.3 us  [body(): full_down = jnp.concatenate(lax.all_to_all(repeated, DP, 0, 0), axis=0)]
    all_gather x1 -> x0, waiting for transfers between devices: 57.5 us -> none  [body(): full_down = lax.all_gather(down_weight, DP, axis=0, tiled=True)]
    all_to_all x1, starting transfers between devices: 9.28 us -> 53.8 us  [sum_in_two_steps(): return jnp.sum(lax.all_to_all(own, far, 0, 0, tiled=True), axis=0)]
    all_to_all x0 -> x1, starting transfers between devices: none -> 16.9 us  [body(): full_down = jnp.concatenate(lax.all_to_all(repeated, DP, 0, 0), axis=0)]
    unnamed x15 -> x16, local copies, waits for them, and re-layouts: 51.6 us -> 34.8 us
    reshape x0 -> x1, local copies, waits for them, and re-layouts: none -> 16.8 us  [body(): full_down = jnp.concatenate(lax.all_to_all(repeated, DP, 0, 0), axis=0)]
    another operation x0 -> x1, local copies, waits for them, and re-layouts: none -> 7.92 us  [body(): repeated = jnp.stack([down_weight] * lax.axis_size(DP))]
  transfers between devices with their start and end apart: 4 -> 4, of which waited for: 3 -> 3; matrix products, arithmetic and copies ran while one was open for 14% -> 11% of each run, Pallas kernels for 0% -> 0%
where the time goes in v1:
time: 714 us; the launch traced here: 712 us
  waiting for transfers between devices  351 us (49%)
  local copies, waits for them, and re-layouts  98.1 us (14%)
  starting transfers between devices  76.5 us (11%)
  blocking collectives  64.7 us (9%)
  other arithmetic  56.5 us (8%)
  matrix products  46.5 us (7%)
  between operations  18 us (3%)
    all_gather x1, waiting for transfers between devices, body(): lax.all_gather(up_weight, DP, axis=0, tiled=True)  251 us
    all_to_all x1, waiting for transfers between devices, body(): full_down = jnp.concatenate(lax.all_to_all(repeated, DP, 0, 0), axis=0)  58.3 us
    psum x5, blocking collectives, one_axis_at_a_time(): shard = lax.psum(shard, axis)  58.1 us
    all_to_all x1, starting transfers between devices, sum_in_two_steps(): return jnp.sum(lax.all_to_all(own, far, 0, 0, tiled=True), axis=0)  53.8 us
    all_to_all x1, waiting for transfers between devices, sent_to_all(): return lax.all_to_all(copies, axis, split_axis=0, concat_axis=0, tiled=True)  40.8 us
    unnamed x16, local copies, waits for them, and re-layouts  34.8 us
    reshape x1, local copies, waits for them, and re-layouts, body(): hutch_terms.reshape(own_rows * lax.axis_size(DP), ff_local // BLOCK, BLOCK)  26.7 us
    reduce_sum x1, other arithmetic, over_copies(): return jnp.sum(everything, axis=0)  18.1 us
  transfers between devices with their start and end apart: 4, of which 3 were waited for; matrix products, arithmetic and copies ran while one was open for 11% of the time, Pallas kernels for 0%

profile of v1, /device:TPU:1, one launch (start us, length us, event | category | flops | bytes accessed | tf_op | source)
XLA Modules:
  0.0 711.7 jit_solution(13795887788868413789)
XLA Ops:
  7.2 0.0 copy-start
  7.2 0.0 all-gather.3.cloned.1.call-start
  7.2 0.7 all-gather.3.cloned.1.call-update
  7.9 7.9 %stack.2 = bf16[128,14,3584]{2,1,0:T(8,128)(2,1)} broadcast(bf16[14,3584]{1,0:T(8,128)(2,1)} %param.12), dimensions={1,2} | broadcast | bytes 12945408 | tf_op jit(solution)/shard_map/stack | solution.py:96
  15.8 16.9 %all-to-all-start = ((bf16[128,14,3584]{2,1,0:T(8,128)(2,1)}), bf16[128,14,3584]{2,1,0:T(8,128)(2,1)}, u32[]{:S(2)}, u32[]{:S(2)}) async-start(bf16[128,14,3584]{2,1,0:T(8,128)(2,1)} %stack.2), calls=%async_computation | async-start | bytes 29360128 | tf_op jit(solution)/shard_map/all_to_all | solution.py:97
  32.8 15.5 %add_convert_fusion = bf16[1792,3584]{0,1:T(8,128)(2,1)} fusion(s32[3584]{0:T(1024)S(1)} %copy-done.3, s32[1792]{0:T(1024)S(1)} %broadcast_multiply_fusion.1), kind=kLoop, calls=%fused_computation.13 | loop fusion | flops 109182976 | bytes 12866560 | tf_op jit(solution)/shard_map/convert_element_type | solution.py:65
  48.3 251.4 %all-gather.3.cloned.1.call-done = bf16[128,14,3584]{2,1,0:T(8,128)(2,1)} async-done(((bf16[1,14,3584]{2,1,0:T(8,128)(2,1)}), bf16[128,14,3584]{2,1,0:T(8,128)(2,1)}) %all-gather.3.cloned.1.call-update) | async-done | bytes 12845072 | tf_op jit(solution)/shard_map/all_gather | solution.py:92
  299.8 16.8 %reshape.54 = bf16[1792,3584]{1,0:T(8,128)(2,1)} reshape(bf16[128,14,3584]{2,1,0:T(8,128)(2,1)} %all-gather.3.cloned.1.call-done) | data formatting | bytes 25690112
  316.6 17.9 %copy.27 = bf16[1792,3584]{0,1:T(8,128)(2,1)} copy(bf16[1792,3584]{1,0:T(8,128)(2,1)} %reshape.54) | data formatting | bytes 25690112
  334.5 15.0 %fusion.10 = f32[128,7168]{1,0:T(8,128)} fusion(bf16[128,1792]{1,0:T(8,128)(2,1)S(1)} %copy-done, bf16[1792,3584]{0,1:T(8,128)(2,1)} %add_convert_fusion, bf16[1792,3584]{0,1:T(8,128)(2,1)} %copy.27), kind=kOutput, calls=%fused_computation.14 | convolution fusion | flops 3339714560 | bytes 29818880 | tf_op jit(solution)/shard_map/dot_general | solution.py:93
  349.5 3.3 multiply_convert_fusion.1
  352.8 58.3 %all-to-all-done = bf16[128,14,3584]{2,1,0:T(8,128)(2,1)} async-done(((bf16[128,14,3584]{2,1,0:T(8,128)(2,1)}), bf16[128,14,3584]{2,1,0:T(8,128)(2,1)}, u32[]{:S(2)}, u32[]{:S(2)}) %all-to-all-start) | async-done | bytes 12845088 | tf_op jit(solution)/shard_map/all_to_all | solution.py:97
  411.0 16.8 %reshape.49 = bf16[1792,3584]{1,0:T(8,128)(2,1)} reshape(bf16[128,14,3584]{2,1,0:T(8,128)(2,1)} %all-to-all-done) | data formatting | bytes 25690112 | tf_op jit(solution)/shard_map/reshape | solution.py:97
  427.8 7.0 fusion.23
  434.8 0.1 fusion.50
  435.0 0.1 reshape.51
  435.0 0.1 reshape.50
  435.1 0.1 pad_maximum_fusion
  435.2 3.3 broadcast_in_dim.2
  438.5 5.7 all-to-all-start.1
  444.3 40.8 %all-to-all-done.1 = f32[2,1,458752]{2,1,0:T(1,128)} async-done(((f32[2,1,458752]{2,1,0:T(1,128)}), f32[2,1,458752]{2,1,0:T(1,128)}, u32[]{:S(2)}, u32[]{:S(2)}) %all-to-all-start.1) | async-done | bytes 3670048 | tf_op jit(solution)/shard_map/all_to_all | solution.py:17
  485.1 18.1 %reduce_sum.54 = f32[458752]{0:T(1024)S(1)} reduce(f32[2,1,458752]{2,1,0:T(1,128)} %all-to-all-done.1, f32[]{:T(128)} %constant.20.clone.1), dimensions={0,1}, to_apply=%region_0.0 | reduce | flops 458752 | bytes 5505028 | tf_op jit(solution)/shard_map/reduce_sum | solution.py:22
  503.2 1.0 fusion.49
  504.3 1.3 slice.49
  505.6 0.2 slice.51
  505.8 2.0 fusion.27
  507.7 6.7 fusion.29
  514.4 17.9 %bitcast_multiply_fusion = f32[1792,3584]{0,1:T(8,128)} fusion(bf16[128,1792]{1,0:T(8,128)(2,1)S(1)} %copy-done, s32[3584]{0:T(1024)S(1)} %copy-done.3, s32[1792]{0:T(1024)S(1)} %broadcast_multiply_fusion.1, f32[256,3584]{1,0:T(8,128)S(1)} %fusion.29, f32[128,7168]{1,0:T(8,128)S(1)} %copy-done.2), kind=kOutput, calls=%fused_computation.12 | convolution fusion | flops 1779957760 | bytes 33510400 | tf_op jit(solution)/shard_map/tr,tf->rf/dot_general | solution.py:118
  532.3 26.7 %reshape.52 = f32[1792,256,14]{0,2,1:T(8,128)} reshape(f32[1792,3584]{0,1:T(8,128)} %bitcast_multiply_fusion) | data formatting | bytes 51380224 | tf_op jit(solution)/shard_map/reshape | solution.py:122
  559.0 13.6 %reduce_sum.55 = f32[1792,256]{0,1:T(8,128)} reduce(f32[1792,256,14]{0,2,1:T(8,128)} %reshape.52, f32[]{:T(128)} %constant.20.clone.1), dimensions={2}, to_apply=%region_1.0 | reduce | flops 5963776 | bytes 27525124 | tf_op jit(solution)/shard_map/reduce_sum | solution.py:122
  572.7 1.7 broadcast_multiply_fusion
  574.3 1.7 copy.29
  576.1 1.6 div.19
  577.6 1.1 copy.30
  578.7 0.0 copy-start.1
  578.7 6.6 all_to_all.21
  585.4 0.2 reduce_sum.56
  585.6 1.5 copy.31
  587.1 53.8 %all-to-all-start.3 = ((f32[64,14,256]{2,1,0:T(8,128)}), f32[64,14,256]{2,1,0:T(8,128)S(1)}, u32[]{:S(2)}, u32[]{:S(2)}) async-start(f32[64,14,256]{2,1,0:T(8,128)} %copy.31), calls=%async_computation.3 | async-start | bytes 2097152 | tf_op jit(solution)/shard_map/all_to_all | solution.py:48
  640.9 0.6 convert_reduce_fusion
  642.8 26.9 %all-reduce.2 = (f32[]{:T(128)}, f32[]{:T(128)}) all-reduce(f32[]{:T(128)S(6)} %mul.184, f32[]{:T(128)S(6)} %mul.191), channel_id=1, replica_groups=mesh['dp_0'=4,'dp_1'=4,'dp_2'=4,'dp_3'=2,'tensor'=2] {'dp_0'}, use_global_device_ids=true, to_apply=%region_5.0 | all-reduce | flops 2 | bytes 16 | tf_op jit(solution)/shard_map/psum | solution.py:53
  669.8 8.9 %all-reduce.1 = (f32[]{:T(128)}, f32[]{:T(128)}) all-reduce(f32[]{:T(128)} %get-tuple-element.7, f32[]{:T(128)} %get-tuple-element.8), channel_id=1, replica_groups=mesh['dp_0'=4,'dp_1'=4,'dp_2'=4,'dp_3'=2,'tensor'=2] {'dp_1'}, use_global_device_ids=true, to_apply=%region_6.0 | all-reduce | flops 2 | bytes 16 | tf_op jit(solution)/shard_map/psum | solution.py:53
  678.7 8.8 %all-reduce = (f32[]{:T(128)}, f32[]{:T(128)}) all-reduce(f32[]{:T(128)} %get-tuple-element.5, f32[]{:T(128)} %get-tuple-element.6), channel_id=1, replica_groups=mesh['dp_0'=4,'dp_1'=4,'dp_2'=4,'dp_3'=2,'tensor'=2] {'dp_2'}, use_global_device_ids=true, to_apply=%region_7.0 | all-reduce | flops 2 | bytes 16 | tf_op jit(solution)/shard_map/psum | solution.py:53
  687.5 8.8 %all-reduce.4 = (f32[]{:T(128)}, f32[]{:T(128)}) all-reduce(f32[]{:T(128)} %get-tuple-element.3, f32[]{:T(128)} %get-tuple-element.4), channel_id=1, replica_groups=mesh['dp_0'=4,'dp_1'=4,'dp_2'=4,'dp_3'=2,'tensor'=2] {'dp_3'}, use_global_device_ids=true, to_apply=%region_8.0 | all-reduce | flops 2 | bytes 16 | tf_op jit(solution)/shard_map/psum | solution.py:53
  696.3 4.6 all-reduce.3
  702.3 0.0 all-to-all-done.3
  702.3 0.1 reduce_sum.57
  702.4 1.3 fusion.39
  (14 shorter events, 0.0 us)
Async XLA Ops:
  7.2 327.3 %copy-start = (bf16[128,1792]{1,0:T(8,128)(2,1)S(1)}, bf16[128,1792]{1,0:T(8,128)(2,1)}, u32[]{:S(2)}) copy-start(bf16[128,1792]{1,0:T(8,128)(2,1)} %param.8) | copy-start | bytes 1376260
  7.2 292.6 %all-gather.3.cloned.1.call-start = ((), (), s32[]{:S(2)}) async-start(), calls=%async_computation.4 | async-start | bytes 14794752 | tf_op jit(solution)/shard_map/all_gather | solution.py:92
  15.8 16.9 %copy-start.5 = (s32[1792]{0:T(1024)S(1)}, s32[1792]{0:T(1024)}, u32[]{:S(2)}) copy-start(s32[1792]{0:T(1024)} %param.13) | copy-start | bytes 21508
  15.8 17.0 %copy-start.3 = (s32[3584]{0:T(1024)S(1)}, s32[3584]{0:T(1024)}, u32[]{:S(2)}) copy-start(s32[3584]{0:T(1024)} %param.14) | copy-start | bytes 43012
  15.8 395.2 %all-to-all-start = ((bf16[128,14,3584]{2,1,0:T(8,128)(2,1)}), bf16[128,14,3584]{2,1,0:T(8,128)(2,1)}, u32[]{:S(2)}, u32[]{:S(2)}) async-start(bf16[128,14,3584]{2,1,0:T(8,128)(2,1)} %stack.2), calls=%async_computation | async-start | bytes 29360128 | tf_op jit(solution)/shard_map/all_to_all | solution.py:97
  438.5 5.7 copy-start.6
  438.5 46.6 %all-to-all-start.1 = ((f32[2,1,458752]{2,1,0:T(1,128)}), f32[2,1,458752]{2,1,0:T(1,128)}, u32[]{:S(2)}, u32[]{:S(2)}) async-start(f32[2,1,458752]{2,1,0:T(1,128)} %broadcast_in_dim.2), calls=%async_computation.1 | async-start | bytes 7340032 | tf_op jit(solution)/shard_map/all_to_all | solution.py:17
  507.7 6.7 copy-start.2
  578.7 125.0 %copy-start.1 = (bf16[128,1792]{1,0:T(8,128)(2,1)S(1)}, bf16[128,1792]{1,0:T(8,128)(2,1)}, u32[]{:S(2)}) copy-start(bf16[128,1792]{1,0:T(8,128)(2,1)} %param.8) | copy-start | bytes 1376260
  585.4 117.0 %copy-start.4 = (f32[14,256]{1,0:T(8,128)S(1)}, f32[14,256]{1,0:T(8,128)}, u32[]{:S(2)}) copy-start(f32[14,256]{1,0:T(8,128)} %param.15) | copy-start | bytes 43012
  587.1 115.2 %all-to-all-start.3 = ((f32[64,14,256]{2,1,0:T(8,128)}), f32[64,14,256]{2,1,0:T(8,128)S(1)}, u32[]{:S(2)}, u32[]{:S(2)}) async-start(f32[64,14,256]{2,1,0:T(8,128)} %copy.31), calls=%async_computation.3 | async-start | bytes 2097152 | tf_op jit(solution)/shard_map/all_to_all | solution.py:48
Sparse Core Ops, SparseCore 0:
  11.4 288.3 all-gather.2
